TPU v7x, 32 devices: a whole 2x2x4 slice. The times are simulated.
32 devices in a mesh: seq: 8 (over z, y), rep: 4 (over x, core).
Axes of the slice: x: 2, y: 2, z: 4, core: 2. Of those that a mesh axis runs over, the one named last changes fastest.
Arguments:
- inputs: bfloat16 [4, 1024, 1024], P('rep', 'seq'), may hold values from -6 to 6
- weight_t: bfloat16 [3072, 1024], P('seq', 'rep'), may hold values from -0.1875 to 0.1875
- states: float32 [4, 1024, 1024], P('rep', 'seq'), may hold values from -0.9 to 0.9
- doc_ids: int32 [4, 1024], P('rep', 'seq'), may hold values from 0 to 3, never falling along the last dimension, each value on 1 to 512 neighbouring positions
- recur: float32 [3, 1024], replicated, may hold values from -1 to 1
- bias: float32 [3, 1024], replicated, may hold values from -8 to 3, as said below
- out_grad: bfloat16 [4, 1024, 1024], P('rep', 'seq'), may hold values from -6 to 6
Outputs:
- input_grad: bfloat16 [4, 1024, 1024], P('rep', 'seq')
- weight_grad: float32 [3072, 1024], P('seq', 'rep')
- param_grad: float32 [6, 1024], replicated
Inputs may be any that keep to these rules, and one draw needn't show every extreme that they name: `doc_ids`: within each sequence the numbers never fall; every document has 1 to 512 tokens, and some document has exactly 512. `bias`: row 0 lies between -8 and -1, rows 1 and 2 between -3 and 3.
All inputs are finite; a program needn't handle non-finite values.
Results may differ from a plain program's by a relative error of at most 0.0095.
Values may be sent and summed in bfloat16 or wider, within the bound.
A program may use at most 128 MiB of HBM per device.

v0:
```python
import math

import jax
import jax.numpy as jnp
from jax import lax
from jax.sharding import PartitionSpec as P


def shifted(block, axis, distance):
    devices = range(lax.axis_size(axis))
    route = [(i - distance, i) for i in devices if i - distance in devices]
    return lax.ppermute(block, axis, route)


def compose(earlier, later):
    return (later[0] * earlier[0], later[1] + later[0] * earlier[1])


def local(inputs, weight_t, states, doc_ids, recur, bias, out_grad):
    feats = inputs[0]
    hidden_now = states[0]
    ids_float = doc_ids[0].astype(jnp.float32)
    count = feats.shape[0]
    width = hidden_now.shape[1]
    columns = lax.all_gather(weight_t, "rep", axis=1, tiled=True)
    contract_last = (((1,), (1,)), ((), ()))
    full_weight = lax.all_gather(columns, "seq", axis=0, tiled=True)
    preact = lax.dot_general(feats, full_weight, contract_last, preferred_element_type=jnp.float32)
    tail_state, tail_id = shifted((hidden_now[-1:], ids_float[-1:]), "seq", 1)
    first_same = jnp.where(
        (ids_float[0] == tail_id[0]) & (lax.axis_index("seq") > 0), 1.0, 0.0
    ).astype(jnp.float32)
    same = jnp.concatenate(
        [first_same[None], (ids_float[1:] == ids_float[:-1]).astype(jnp.float32)]
    )
    prior = jnp.concatenate([tail_state, hidden_now[:-1]], 0) * same[:, None]
    gate_z = jax.nn.sigmoid(preact[:, :width] + recur[0] * prior + bias[0])
    gate_r = jax.nn.sigmoid(preact[:, width : 2 * width] + recur[1] * prior + bias[1])
    gate_c = jnp.tanh(preact[:, 2 * width :] + recur[2] * gate_r * prior + bias[2])
    jacobian = same[:, None] * (
        1.0
        - gate_z
        + (gate_c - prior) * gate_z * (1.0 - gate_z) * recur[0]
        + gate_z
        * (1.0 - gate_c * gate_c)
        * recur[2]
        * (gate_r + prior * gate_r * (1.0 - gate_r) * recur[1])
    )
    upstream = out_grad[0].astype(jnp.float32)
    jac_rows, up_rows = (
        lax.all_to_all(jacobian.T, "seq", split_axis=0, concat_axis=1, tiled=True),
        lax.all_to_all(upstream.T, "seq", split_axis=0, concat_axis=1, tiled=True),
    )
    factor = jnp.concatenate([jac_rows[:, 1:], jnp.zeros((jac_rows.shape[0], 1), jnp.float32)], 1)
    _, adjoint_rows = lax.associative_scan(compose, (factor, up_rows), reverse=True, axis=1)
    adjoint = lax.all_to_all(adjoint_rows, "seq", split_axis=1, concat_axis=0, tiled=True).T
    grad_z = adjoint * (gate_c - prior) * gate_z * (1.0 - gate_z)
    grad_c = adjoint * gate_z * (1.0 - gate_c * gate_c)
    grad_r = grad_c * recur[2] * prior * gate_r * (1.0 - gate_r)
    grad_pre = jnp.concatenate([grad_z, grad_r, grad_c], 1).astype(jnp.bfloat16)
    input_grad = jnp.dot(grad_pre, full_weight, preferred_element_type=jnp.float32)
    tokens_all = count * inputs.shape[0] * lax.axis_size("seq") * lax.axis_size("rep")
    normal_factor = 1.0 / math.sqrt(tokens_all)
    row_share = lax.psum_scatter(
        lax.dot_general(
            grad_pre, feats, (((0,), (0,)), ((), ())), preferred_element_type=jnp.float32
        ),
        "seq",
        scatter_dimension=0,
        tiled=True,
    )
    weight_grad = (
        lax.psum_scatter(
            row_share.astype(jnp.bfloat16), "rep", scatter_dimension=1, tiled=True
        ).astype(jnp.float32)
        * normal_factor
    )
    stats = jnp.stack(
        [
            grad_z.sum(0),
            grad_r.sum(0),
            grad_c.sum(0),
            (grad_z * prior).sum(0),
            (grad_r * prior).sum(0),
            (grad_c * gate_r * prior).sum(0),
        ]
    )
    param_grad = lax.psum(stats, ("seq", "rep")) * normal_factor
    return (input_grad.astype(jnp.bfloat16)[None], weight_grad, param_grad)


def solution(mesh):
    placed = (
        P("rep", "seq", None),
        P("seq", "rep"),
        P("rep", "seq", None),
        P("rep", "seq"),
        P(),
        P(),
        P("rep", "seq", None),
    )
    return jax.shard_map(
        local,
        mesh=mesh,
        in_specs=placed,
        out_specs=(P("rep", "seq", None), P("seq", "rep"), P()),
        check_vma=False,
    )
```

profile of v0, /device:TPU:27, one launch (start us, length us, event | category | flops | bytes accessed | tf_op | source)
XLA Modules:
  0.0 487.7 jit_solution(18385137196122489823)
XLA Ops:
  7.3 9.9 %all_gather.6 = bf16[384,1024]{1,0:T(8,128)(2,1)} all-gather(bf16[384,256]{1,0:T(8,128)(2,1)} %param.8), channel_id=1, replica_groups=mesh['seq'=8,'rep'=4] {'rep'}, dimensions={1}, use_global_device_ids=true | all-gather | bytes 983040 | tf_op jit(solution)/shard_map/all_gather | solution.py:25
  17.8 3.1 collective-permute-start
  21.0 1.9 collective-permute-start.1
  24.0 5.7 %all-to-all-start = ((f32[8,128,128]{2,1,0:T(8,128)}), f32[8,128,128]{2,1,0:T(8,128)S(1)}, u32[]{:S(2)}, u32[]{:S(2)}) async-start(f32[8,128,128]{2,1,0:T(8,128)} %bitcast.2), calls=%async_computation | async-start | bytes 1048576 | tf_op jit(solution)/shard_map/all_to_all | solution.py:52
  31.2 94.6 %all-gather.2.cloned.1.call-done = bf16[3072,1024]{1,0:T(8,128)(2,1)} async-done(((bf16[384,1024]{1,0:T(8,128)(2,1)}), bf16[3072,1024]{1,0:T(8,128)(2,1)}) %all-gather.2.cloned.1.call-update) | async-done | bytes 6291472 | tf_op jit(solution)/shard_map/all_gather | solution.py:27
  125.9 5.0 %fusion.21 = f32[128,3072]{1,0:T(8,128)S(1)} fusion(bf16[3072,1024]{1,0:T(8,128)(2,1)} %all-gather.2.cloned.1.call-done, bf16[1,128,1024]{2,1,0:T(8,128)(2,1)S(1)} %copy-done), kind=kOutput, calls=%fused_computation.40 | convolution fusion | flops 805306368 | bytes 8126464 | tf_op jit(solution)/shard_map/dot_general | solution.py:28
  130.9 1.6 copy_bitcast_fusion
  132.5 4.8 all-to-all-start.1
  137.5 1.4 slice.317
  140.2 1.9 slice.318
  142.1 1.3 slice.342
  144.7 4.0 all-to-all-done.1
  149.9 1.4 slice.339
  151.3 1.4 slice.343
  153.0 2.9 slice.344
  179.8 1.9 slice.340
  196.5 3.4 rev.2
  199.9 17.9 %all_to_all.63 = f32[128,8,128]{0,2,1:T(8,128)S(1)} all-to-all(f32[128,8,128]{0,2,1:T(8,128)S(1)} %bitcast.86), channel_id=1, replica_groups=mesh['seq'=8,'rep'=4] {'seq'}, dimensions={1} | all-to-all | bytes 1048576 | tf_op jit(solution)/shard_map/all_to_all | solution.py:56
  218.8 6.3 %fusion.18 = f32[3072,1024]{1,0:T(8,128)} fusion(bf16[128,1024]{1,0:T(8,128)(2,1)S(1)} %get-tuple-element.11, bf16[128,1024]{1,0:T(8,128)(2,1)S(1)} %get-tuple-element.10, bf16[128,1024]{1,0:T(8,128)(2,1)S(1)} %get-tuple-element.9, bf16[1,128,1024]{2,1,0:T(8,128)(2,1)S(1)} %copy-done), kind=kOutput, calls=%fused_computation.34 | convolution fusion | flops 807665664 | bytes 13631488 | tf_op jit(solution)/shard_map/dot_general | solution.py:65
  225.2 207.5 %reduce-scatter.3.cloned.1.call-done = f32[384,1024]{1,0:T(8,128)} async-done(((f32[3072,1024]{1,0:T(8,128)}), f32[384,1024]{1,0:T(8,128)}) %reduce-scatter.3.cloned.1.call-update) | async-done | bytes 1572880 | tf_op jit(solution)/shard_map/reduce_scatter | solution.py:64
  432.7 2.4 convert_element_type.29
  435.2 39.2 %psum.7 = f32[6,1024]{1,0:T(8,128)S(1)} all-reduce(f32[6,1024]{1,0:T(8,128)S(1)} %stack.27), channel_id=1, replica_groups=mesh['seq'=8,'rep'=4] {'seq','rep'}, use_global_device_ids=true, to_apply=%region_8.9 | all-reduce | flops 6144 | bytes 49152 | tf_op jit(solution)/shard_map/psum | solution.py:88
  475.0 4.5 fusion
  479.5 1.7 convert_multiply_fusion
  (191 shorter events, 46.3 us)
Async XLA Ops:
  7.2 118.7 %copy-start = (bf16[1,128,1024]{2,1,0:T(8,128)(2,1)S(1)}, bf16[1,128,1024]{2,1,0:T(8,128)(2,1)}, u32[]{:S(2)}) copy-start(bf16[1,128,1024]{2,1,0:T(8,128)(2,1)} %param.7) | copy-start | bytes 786436
  7.2 15.7 %copy-start.2 = (bf16[1,128,1024]{2,1,0:T(8,128)(2,1)S(1)}, bf16[1,128,1024]{2,1,0:T(8,128)(2,1)}, u32[]{:S(2)}) copy-start(bf16[1,128,1024]{2,1,0:T(8,128)(2,1)} %param.13) | copy-start | bytes 786436
  7.2 118.6 %all-gather.2.cloned.1.call-start = ((), (), s32[]{:S(2)}) async-start(), calls=%async_computation.5 | async-start | bytes 7077888 | tf_op jit(solution)/shard_map/all_gather | solution.py:27
  17.8 12.1 %collective-permute-start = (f32[1]{0:T(128)}, f32[1]{0:T(128)}, u32[]{:S(2)}, u32[]{:S(2)}) collective-permute-start(f32[1]{0:T(128)} %bitcast.6), channel_id=1, source_target_pairs={{0,4},{4,8},{8,12},{12,16},{16,20},{20,24},{24,28},{1,5},{5,9},{9,... | collective-permute-start | bytes 20 | tf_op jit(solution)/shard_map/ppermute | solution.py:12
  21.0 109.8 %collective-permute-start.1 = (f32[1,1024]{1,0:T(1,128)S(1)}, f32[1,1024]{1,0:T(1,128)S(1)}, u32[]{:S(2)}, u32[]{:S(2)}) collective-permute-start(f32[1,1024]{1,0:T(1,128)S(1)} %slice_bitcast_fusion.1), channel_id=1, source_target_pairs={{0,4},{4,8},{8,12},{12,16},{16,20},{20,24},{24,28},{1,5},{5,9},{9,... | collective-permute-start | bytes 12296 | tf_op jit(solution)/shard_map/ppermute | solution.py:12
  24.0 108.6 %all-to-all-start = ((f32[8,128,128]{2,1,0:T(8,128)}), f32[8,128,128]{2,1,0:T(8,128)S(1)}, u32[]{:S(2)}, u32[]{:S(2)}) async-start(f32[8,128,128]{2,1,0:T(8,128)} %bitcast.2), calls=%async_computation | async-start | bytes 1048576 | tf_op jit(solution)/shard_map/all_to_all | solution.py:52
  29.7 101.2 %copy-start.3 = (f32[1,1024]{1,0:T(1,128)}, f32[1,1024]{1,0:T(1,128)S(1)}, u32[]{:S(2)}) copy-start(f32[1,1024]{1,0:T(1,128)S(1)} %get-tuple-element.25) | copy-start | bytes 12292
  29.7 101.2 %copy-start.5 = (f32[1,1024]{1,0:T(1,128)}, f32[1,1024]{1,0:T(1,128)S(1)}, u32[]{:S(2)}) copy-start(f32[1,1024]{1,0:T(1,128)S(1)} %get-tuple-element.26) | copy-start | bytes 12292
  29.7 101.2 %copy-start.7 = (f32[1,1024]{1,0:T(1,128)}, f32[1,1024]{1,0:T(1,128)S(1)}, u32[]{:S(2)}) copy-start(f32[1,1024]{1,0:T(1,128)S(1)} %get-tuple-element.27) | copy-start | bytes 12292
  29.7 101.1 %copy-start.9 = (f32[1,1024]{1,0:T(1,128)}, f32[1,1024]{1,0:T(1,128)S(1)}, u32[]{:S(2)}) copy-start(f32[1,1024]{1,0:T(1,128)S(1)} %get-tuple-element.22) | copy-start | bytes 12292
  29.7 101.1 %copy-start.11 = (f32[1,1024]{1,0:T(1,128)}, f32[1,1024]{1,0:T(1,128)S(1)}, u32[]{:S(2)}) copy-start(f32[1,1024]{1,0:T(1,128)S(1)} %get-tuple-element.23) | copy-start | bytes 12292
  29.8 101.1 %copy-start.13 = (f32[1,1024]{1,0:T(1,128)}, f32[1,1024]{1,0:T(1,128)S(1)}, u32[]{:S(2)}) copy-start(f32[1,1024]{1,0:T(1,128)S(1)} %get-tuple-element.24) | copy-start | bytes 12292
  31.2 99.7 %copy-start.19 = (f32[128]{0:T(128)}, f32[128]{0:T(128)S(1)}, u32[]{:S(2)}) copy-start(f32[128]{0:T(128)S(1)} %pad_maximum_fusion.12) | copy-start | bytes 1540
  132.5 16.2 %all-to-all-start.1 = ((f32[8,128,128]{1,2,0:T(8,128)}), f32[8,128,128]{1,2,0:T(8,128)}, u32[]{:S(2)}, u32[]{:S(2)}) async-start(f32[8,128,128]{1,2,0:T(8,128)} %copy_bitcast_fusion), calls=%async_computation.1 | async-start | bytes 1048576 | tf_op jit(solution)/shard_map/all_to_all | solution.py:51
  137.3 295.4 %reduce-scatter.3.cloned.1.call-start = ((), (), s32[]{:S(2)}) async-start(), calls=%async_computation.6 | async-start | bytes 14155776 | tf_op jit(solution)/shard_map/reduce_scatter | solution.py:64
  195.5 22.2 %copy-start.4 = (f32[1,1024]{1,0:T(1,128)S(1)}, f32[1,1024]{1,0:T(1,128)}, u32[]{:S(2)}) copy-start(f32[1,1024]{1,0:T(1,128)} %copy-done.3) | copy-start | bytes 12292
  195.5 22.2 %copy-start.6 = (f32[1,1024]{1,0:T(1,128)S(1)}, f32[1,1024]{1,0:T(1,128)}, u32[]{:S(2)}) copy-start(f32[1,1024]{1,0:T(1,128)} %copy-done.5) | copy-start | bytes 12292
  195.5 22.2 %copy-start.8 = (f32[1,1024]{1,0:T(1,128)S(1)}, f32[1,1024]{1,0:T(1,128)}, u32[]{:S(2)}) copy-start(f32[1,1024]{1,0:T(1,128)} %copy-done.7) | copy-start | bytes 12292
  195.6 22.2 %copy-start.10 = (f32[1,1024]{1,0:T(1,128)S(1)}, f32[1,1024]{1,0:T(1,128)}, u32[]{:S(2)}) copy-start(f32[1,1024]{1,0:T(1,128)} %copy-done.9) | copy-start | bytes 12292
  195.6 22.2 %copy-start.12 = (f32[1,1024]{1,0:T(1,128)S(1)}, f32[1,1024]{1,0:T(1,128)}, u32[]{:S(2)}) copy-start(f32[1,1024]{1,0:T(1,128)} %copy-done.11) | copy-start | bytes 12292
  195.6 22.2 %copy-start.14 = (f32[1,1024]{1,0:T(1,128)S(1)}, f32[1,1024]{1,0:T(1,128)}, u32[]{:S(2)}) copy-start(f32[1,1024]{1,0:T(1,128)} %copy-done.13) | copy-start | bytes 12292
  195.6 22.2 %copy-start.16 = (f32[1,1024]{1,0:T(1,128)S(1)}, f32[1,1024]{1,0:T(1,128)}, u32[]{:S(2)}) copy-start(f32[1,1024]{1,0:T(1,128)} %copy-done.15) | copy-start | bytes 12292
  195.6 22.2 %copy-start.20 = (f32[128]{0:T(128)S(1)}, f32[128]{0:T(128)}, u32[]{:S(2)}) copy-start(f32[128]{0:T(128)} %copy-done.19) | copy-start | bytes 1540
  225.2 254.3 %reduce-scatter.5.cloned.1.call-start = ((), (), s32[]{:S(2)}) async-start(), calls=%async_computation.7 | async-start | bytes 983040 | tf_op jit(solution)/shard_map/reduce_scatter | solution.py:73
  (8 other events, 69.6 us)
Sparse Core Ops, SparseCore 0:
  17.3 108.4 all-gather.1
  225.3 207.3 reduce-scatter.2
  435.3 22.9 reduce-scatter.4
where the time goes:
time: 493 us; the launch traced here: 488 us
  waiting for transfers between devices  306 us (62%)
  blocking collectives  66.9 us (14%)
  local copies, waits for them, and re-layouts  42.2 us (9%)
  other arithmetic  25.3 us (5%)
  matrix products  15.8 us (3%)
  between operations  15.7 us (3%)
  starting transfers between devices  15.6 us (3%)
    reduce_scatter x1, waiting for transfers between devices, local(): lax.psum_scatter(lax.dot_general(grad_pre, feats, (((0,), (0,)), ((), ())...  208 us
    all_gather x1, waiting for transfers between devices, local(): full_weight = lax.all_gather(columns, 'seq', axis=0, tiled=True)  94.6 us
    psum x1, blocking collectives, local(): param_grad = lax.psum(stats, ('seq', 'rep')) * normal_factor  39.2 us
    slice x66, local copies, waits for them, and re-layouts, local(): lax.associative_scan(compose, (factor, up_rows), reverse=True, axis=1)  33.1 us
    all_to_all x1, blocking collectives, local(): lax.all_to_all(adjoint_rows, 'seq', split_axis=1, concat_axis=0, tiled=True)  17.9 us
    all_gather x1, blocking collectives, local(): columns = lax.all_gather(weight_t, 'rep', axis=1, tiled=True)  9.93 us
  transfers between devices with their start and end apart: 7, of which 3 were waited for; matrix products, arithmetic and copies ran while one was open for 4% of the time, Pallas kernels for 0%

commit v1 on v0

v1 whole, which is shorter than its diff:
```python
import functools
import math

import jax
import jax.numpy as jnp
from jax import lax
from jax.experimental import pallas as pl
from jax.experimental.pallas import tpu as pltpu
from jax.sharding import PartitionSpec as P

F32 = jnp.float32
BF16 = jnp.bfloat16
GATES = 3


def shifted(block, axis, distance):
    devices = range(lax.axis_size(axis))
    route = [(i - distance, i) for i in devices if i - distance in devices]
    return lax.ppermute(block, axis, route)


def compose(earlier, later):
    return (later[0] * earlier[0], later[1] + later[0] * earlier[1])


def by_tokens(inputs, weight_t, states, doc_ids, recur, bias, out_grad):
    feats = inputs[0]
    hidden_now = states[0]
    ids_float = doc_ids[0].astype(F32)
    count = feats.shape[0]
    width = hidden_now.shape[1]
    columns = lax.all_gather(weight_t, "rep", axis=1, tiled=True)
    contract_last = (((1,), (1,)), ((), ()))
    full_weight = lax.all_gather(columns, "seq", axis=0, tiled=True)
    preact = lax.dot_general(feats, full_weight, contract_last, preferred_element_type=F32)
    tail_state, tail_id = shifted((hidden_now[-1:], ids_float[-1:]), "seq", 1)
    first_same = jnp.where(
        (ids_float[0] == tail_id[0]) & (lax.axis_index("seq") > 0), 1.0, 0.0
    ).astype(F32)
    same = jnp.concatenate([first_same[None], (ids_float[1:] == ids_float[:-1]).astype(F32)])
    prior = jnp.concatenate([tail_state, hidden_now[:-1]], 0) * same[:, None]
    gate_z = jax.nn.sigmoid(preact[:, :width] + recur[0] * prior + bias[0])
    gate_r = jax.nn.sigmoid(preact[:, width : 2 * width] + recur[1] * prior + bias[1])
    gate_c = jnp.tanh(preact[:, 2 * width :] + recur[2] * gate_r * prior + bias[2])
    jacobian = same[:, None] * (
        1.0
        - gate_z
        + (gate_c - prior) * gate_z * (1.0 - gate_z) * recur[0]
        + gate_z
        * (1.0 - gate_c * gate_c)
        * recur[2]
        * (gate_r + prior * gate_r * (1.0 - gate_r) * recur[1])
    )
    upstream = out_grad[0].astype(F32)
    jac_rows, up_rows = (
        lax.all_to_all(jacobian.T, "seq", split_axis=0, concat_axis=1, tiled=True),
        lax.all_to_all(upstream.T, "seq", split_axis=0, concat_axis=1, tiled=True),
    )
    factor = jnp.concatenate([jac_rows[:, 1:], jnp.zeros((jac_rows.shape[0], 1), F32)], 1)
    _, adjoint_rows = lax.associative_scan(compose, (factor, up_rows), reverse=True, axis=1)
    adjoint = lax.all_to_all(adjoint_rows, "seq", split_axis=1, concat_axis=0, tiled=True).T
    grad_z = adjoint * (gate_c - prior) * gate_z * (1.0 - gate_z)
    grad_c = adjoint * gate_z * (1.0 - gate_c * gate_c)
    grad_r = grad_c * recur[2] * prior * gate_r * (1.0 - gate_r)
    grad_pre = jnp.concatenate([grad_z, grad_r, grad_c], 1).astype(BF16)
    input_grad = jnp.dot(grad_pre, full_weight, preferred_element_type=F32)
    tokens_all = count * inputs.shape[0] * lax.axis_size("seq") * lax.axis_size("rep")
    normal_factor = 1.0 / math.sqrt(tokens_all)
    row_share = lax.psum_scatter(
        lax.dot_general(grad_pre, feats, (((0,), (0,)), ((), ())), preferred_element_type=F32),
        "seq",
        scatter_dimension=0,
        tiled=True,
    )
    weight_grad = (
        lax.psum_scatter(row_share.astype(BF16), "rep", scatter_dimension=1, tiled=True).astype(F32)
        * normal_factor
    )
    stats = jnp.stack(
        [
            grad_z.sum(0),
            grad_r.sum(0),
            grad_c.sum(0),
            (grad_z * prior).sum(0),
            (grad_r * prior).sum(0),
            (grad_c * gate_r * prior).sum(0),
        ]
    )
    param_grad = lax.psum(stats, ("seq", "rep")) * normal_factor
    return (input_grad.astype(BF16)[None], weight_grad, param_grad)


def swap_roles(a, b):
    return 2 * (a // 2) + b % 2, 2 * (b // 2) + a % 2


def kernel(
    ns, nr, feats, weight, states, ids, recur, bias, upstream,
    out_in, out_w, out_p,
    pay_src, pay, ids_src, ids_all, x_all, w_all, prev, ids_col, up, jac, co_z, co_r, co_c, rprior,
    scan_a, scan_b, carry, lam, grads, part_out, part_in, part_keep, fin_out, fin_in, wg_out, wg_in,
    st_out, st_in,
    x_s0, x_sz, x_sd, x_r, w_s1, w_s2, w_r, p_s, p_r, i_s, i_r, d_s, d_r, f_s, f_r, g_s, g_r, t_s, t_r,
):
    T, DI = feats.shape
    H = states.shape[1]
    hb, cw, nz = H // ns, DI // nr, ns // 2
    s, r = lax.axis_index("seq"), lax.axis_index("rep")
    k, q = swap_roles(s, r)
    z, c = k // 2, k % 2
    me = s * nr + r
    unsent = []

    def place(a, b):
        return {"seq": a, "rep": b}

    def send(src, dst, ssem, rsem, where):
        pltpu.make_async_remote_copy(
            src_ref=src, dst_ref=dst, send_sem=ssem, recv_sem=rsem,
            device_id=where, device_id_type=pl.DeviceIdType.MESH,
        ).start()

    def local(src, dst, rsem):
        pltpu.make_async_copy(src, dst, rsem).start()

    def landed(dst, sem):
        pltpu.make_async_copy(dst, dst, sem).wait()

    def send_or_local(src, dst, ssem, rsem, where, here):
        @pl.when(jnp.logical_not(here))
        def _():
            send(src, dst, ssem, rsem, place(*where))

        @pl.when(here)
        def _():
            local(src, dst, rsem)

        unsent.append((jnp.logical_not(here), src, ssem))

    def rows(ref, block, count):
        return ref.at[pl.ds(pl.multiple_of(block * count, count), count), :]

    for j in range(ns):
        pay_src[j, :, :hb] = states[:, j * hb : (j + 1) * hb].astype(BF16)
        pay_src[j, :, hb:] = upstream[:, j * hb : (j + 1) * hb]
    ids_src[...] = jnp.broadcast_to(ids[...].astype(F32), ids_src.shape)

    barrier = pltpu.get_barrier_semaphore()

    def greet(d, _):
        @pl.when(d != me)
        def _():
            pl.semaphore_signal(
                barrier, inc=1, device_id=place(d // nr, d % nr), device_id_type=pl.DeviceIdType.MESH
            )

        return 0

    lax.fori_loop(0, ns * nr, greet, 0)
    pl.semaphore_wait(barrier, ns * nr - 1)

    diagonal = (s % 2) == (r % 2)
    send_or_local(feats, rows(x_all, s, T), x_s0, x_r.at[s], swap_roles(s, r), diagonal)
    for i in range(GATES):
        b = GATES * s + i
        g, j = b // ns, b % ns
        dst = w_all.at[
            pl.ds(pl.multiple_of(g * hb, hb), hb), pl.ds(pl.multiple_of(r * cw, cw), cw)
        ]
        send_or_local(
            weight.at[i * hb : (i + 1) * hb, :], dst, w_s1.at[i], w_r.at[g * nr + r],
            (2 * (j // 2) + s % 2, 2 * (r // 2) + j % 2), j == k,
        )
    for j in range(ns):
        here = jnp.logical_and(diagonal, k == j)
        where = swap_roles(j, r)
        send_or_local(ids_src, ids_all.at[s], i_s.at[j], i_r.at[s], where, here)
        send_or_local(pay_src.at[j], pay.at[s], p_s.at[j], p_r.at[s], where, here)

    mine = rows(x_all, k, T)
    landed(mine, x_r.at[k])
    for other in range(nz):
        away = other != z

        @pl.when(away)
        def _():
            send(mine, mine, x_sz.at[other], x_r.at[k], place(*swap_roles(2 * other + c, q)))

        unsent.append((away, mine, x_sz.at[other]))
    partner = place(*swap_roles(k + 1 - 2 * c, q))
    send(mine, mine, x_sd.at[z], x_r.at[k], partner)

    def weight_slot(g, col):
        return w_all.at[g * hb : (g + 1) * hb, col * cw : (col + 1) * cw]

    relays = {}
    for g in range(GATES):
        for col in range(nr):
            relay = jnp.logical_and(((g * ns + k) // GATES) % 2 == s % 2, r // 2 == col // 2)
            relays[g, col] = relay
            slot = weight_slot(g, col)

            @pl.when(relay)
            def _():
                landed(slot, w_r.at[g * nr + col])

            for other in range(nr):
                away = jnp.logical_and(relay, q != other)
                sem = w_s2.at[(g * nr + col) * nr + other]

                @pl.when(away)
                def _():
                    send(slot, slot, sem, w_r.at[g * nr + col], place(*swap_roles(k, other)))

                unsent.append((away, slot, sem))

    for other in range(nz):
        block = 2 * other + c
        there = rows(x_all, block, T)

        @pl.when(other != z)
        def _():
            landed(there, x_r.at[block])
            send(there, there, x_sd.at[other], x_r.at[block], partner)

        unsent.append((None, there, x_sd.at[other]))

    prev[0:8, :] = jnp.zeros((8, hb), F32)
    ids_col[0:8, :] = jnp.full((8, hb), -1.0, F32)
    jac[ns * T : ns * T + 8, :] = jnp.zeros((8, hb), F32)
    for m in range(ns):
        landed(ids_all.at[m], i_r.at[m])
        landed(pay.at[m], p_r.at[m])
        prev[8 + m * T : 8 + (m + 1) * T, :] = pay[m, :, :hb].astype(F32)
        up[m * T : (m + 1) * T, :] = pay[m, :, hb:].astype(F32)
        ids_col[8 + m * T : 8 + (m + 1) * T, :] = jnp.broadcast_to(ids_all[m, 0:1, :], (hb, T)).T

    for other in range(nz):
        block = 2 * other + 1 - c
        landed(rows(x_all, block, T), x_r.at[block])
    for g in range(GATES):
        for col in range(nr):

            @pl.when(jnp.logical_not(relays[g, col]))
            def _():
                landed(weight_slot(g, col), w_r.at[g * nr + col])

    group = pl.ds(pl.multiple_of(k * hb, hb), hb)
    rz, rr, rc = (recur[i : i + 1, group] for i in range(GATES))
    bz, br, bc = (bias[i : i + 1, group] for i in range(GATES))
    for m in range(ns):
        span = slice(m * T, (m + 1) * T)
        pre = lax.dot_general(
            x_all[span, :], w_all[...], (((1,), (1,)), ((), ())), preferred_element_type=F32
        )
        same = jnp.where(
            ids_col[8 + m * T : 8 + (m + 1) * T, :] == ids_col[7 + m * T : 7 + (m + 1) * T, :], 1.0, 0.0
        )
        prior = prev[7 + m * T : 7 + (m + 1) * T, :] * same
        gz = jax.nn.sigmoid(pre[:, :hb] + rz * prior + bz)
        gr = jax.nn.sigmoid(pre[:, hb : 2 * hb] + rr * prior + br)
        rp = gr * prior
        gc = jnp.tanh(pre[:, 2 * hb :] + rc * rp + bc)
        az = (gc - prior) * gz * (1.0 - gz)
        ac = gz * (1.0 - gc * gc)
        slope = rp * (1.0 - gr)
        acr = ac * rc
        co_z[span, :] = az
        co_c[span, :] = ac
        co_r[span, :] = acr * slope
        rprior[span, :] = rp
        jac[span, :] = same * (1.0 - gz + az * rz + acr * (gr + slope * rr))

    def back(i, state):
        a, b = state
        t = T - 1 - i
        f = jac[pl.ds(t + 1, ns, stride=T), :]
        u = up[pl.ds(t, ns, stride=T), :]
        a, b = f * a, u + f * b
        scan_a[t] = a
        scan_b[t] = b
        return a, b

    a, b = lax.fori_loop(0, T, back, (jnp.ones((ns, hb), F32), jnp.zeros((ns, hb), F32)), unroll=8)
    tail = jnp.zeros((1, hb), F32)
    for m in reversed(range(ns)):
        carry[m : m + 1, :] = tail
        tail = b[m : m + 1, :] + a[m : m + 1, :] * tail
    carried = carry[...]

    def finish(t, _):
        lam[pl.ds(t, ns, stride=T), :] = scan_b[t] + scan_a[t] * carried
        return 0

    lax.fori_loop(0, T, finish, 0, unroll=8)

    sums = [jnp.zeros((1, hb), F32) for _ in range(6)]
    for m in range(ns):
        span = slice(m * T, (m + 1) * T)
        same = jnp.where(
            ids_col[8 + m * T : 8 + (m + 1) * T, :] == ids_col[7 + m * T : 7 + (m + 1) * T, :], 1.0, 0.0
        )
        prior = prev[7 + m * T : 7 + (m + 1) * T, :] * same
        adj = lam[span, :]
        grad_z = adj * co_z[span, :]
        grad_r = adj * co_r[span, :]
        grad_c = adj * co_c[span, :]
        grads[span, :hb] = grad_z.astype(BF16)
        grads[span, hb : 2 * hb] = grad_r.astype(BF16)
        grads[span, 2 * hb :] = grad_c.astype(BF16)
        terms = (grad_z, grad_r, grad_c, grad_z * prior, grad_r * prior, grad_c * rprior[span, :])
        sums = [total + jnp.sum(term, 0, keepdims=True) for total, term in zip(sums, terms)]
    for i in range(6):
        st_out[i : i + 1, :] = sums[i]
    st_out[6:8, :] = jnp.zeros((2, hb), F32)

    for other in range(nz):
        block = 2 * other + 1 - c
        part_out[other] = jnp.dot(
            rows(grads, block, T)[...], w_all[...], preferred_element_type=F32
        ).astype(BF16)
        send(part_out.at[other], part_in.at[other], d_s.at[other], d_r.at[other], partner)
        unsent.append((None, part_out.at[other], d_s.at[other]))
    for other in range(nz):
        part_keep[other] = jnp.dot(
            rows(grads, 2 * other + c, T)[...], w_all[...], preferred_element_type=F32
        )

    for other in range(nz):
        landed(part_in.at[other], d_r.at[other])
        fin_out[other] = (part_keep[other] + part_in[other].astype(F32)).astype(BF16)
        block = 2 * other + c
        here = jnp.logical_and(block == s, q == r)
        send_or_local(fin_out.at[other], fin_in.at[z], f_s.at[other], f_r.at[z], (block, q), here)

    slot = k * nr + q
    st_in[slot] = st_out[...]

    def tell(d, _):
        @pl.when(d != me)
        def _():
            send(st_out, st_in.at[slot], t_s.at[d], t_r.at[slot], place(d // nr, d % nr))

        return 0

    lax.fori_loop(0, ns * nr, tell, 0)

    for g in range(GATES):
        wg_out[g] = lax.dot_general(
            grads[:, g * hb : (g + 1) * hb], x_all[...], (((0,), (0,)), ((), ())),
            preferred_element_type=F32,
        ).astype(BF16)
        b = g * ns + k
        owner, i = b // GATES, b % GATES
        for col in range(nr):
            here = jnp.logical_and(owner == s, r == col)
            send_or_local(
                wg_out.at[g, :, col * cw : (col + 1) * cw], wg_in.at[q * GATES + i],
                g_s.at[g * nr + col], g_r.at[q * GATES + i], (owner, col), here,
            )

    scale = 1.0 / math.sqrt(ns * nr * T)
    total = None
    for other in range(nz):
        landed(fin_in.at[other], f_r.at[other])
        term = fin_in[other].astype(F32)
        total = term if total is None else total + term
    out_in[...] = total.astype(BF16)

    def heard(d, _):
        @pl.when(d != slot)
        def _():
            landed(st_in.at[d], t_r.at[d])

        return 0

    lax.fori_loop(0, ns * nr, heard, 0)
    for j in range(ns):
        total = st_in[j * nr]
        for other in range(1, nr):
            total = total + st_in[j * nr + other]
        out_p[:, j * hb : (j + 1) * hb] = total[:6] * scale

    for i in range(GATES):
        total = None
        for other in range(nr):
            landed(wg_in.at[other * GATES + i], g_r.at[other * GATES + i])
            term = wg_in[other * GATES + i].astype(F32)
            total = term if total is None else total + term
        out_w[i * hb : (i + 1) * hb, :] = total * scale

    def told(d, _):
        @pl.when(d != me)
        def _():
            landed(st_out, t_s.at[d])

        return 0

    lax.fori_loop(0, ns * nr, told, 0)
    for sent, src, sem in unsent:
        if sent is None:
            landed(src, sem)
        else:

            @pl.when(sent)
            def _():
                landed(src, sem)


def by_hidden(ns, nr, inputs, weight_t, states, doc_ids, recur, bias, out_grad):
    T, DI = inputs.shape[1:]
    H = states.shape[2]
    hb, cw, nz = H // ns, DI // nr, ns // 2
    L = ns * T
    vm = pltpu.VMEM
    scratch = [
        vm((ns, T, 2 * hb), BF16),
        vm((ns, T, 2 * hb), BF16),
        vm((8, T), F32),
        vm((ns, 8, T), F32),
        vm((L, DI), BF16),
        vm((GATES * hb, DI), BF16),
        vm((L + 8, hb), F32),
        vm((L + 8, hb), F32),
        vm((L, hb), F32),
        vm((L + 8, hb), F32),
        vm((L, hb), F32),
        vm((L, hb), F32),
        vm((L, hb), F32),
        vm((L, hb), F32),
        vm((T, ns, hb), F32),
        vm((T, ns, hb), F32),
        vm((ns, hb), F32),
        vm((L, hb), F32),
        vm((L, GATES * hb), BF16),
        vm((nz, T, DI), BF16),
        vm((nz, T, DI), BF16),
        vm((nz, T, DI), F32),
        vm((nz, T, DI), BF16),
        vm((nz, T, DI), BF16),
        vm((GATES, hb, DI), BF16),
        vm((nr * GATES, hb, cw), BF16),
        vm((8, hb), F32),
        vm((ns * nr, 8, hb), F32),
    ]
    dma = pltpu.SemaphoreType.DMA
    counts = [
        None, nz, nz, ns, GATES, GATES * nr * nr, GATES * nr, ns, ns, ns, ns, nz, nz, nz, nz,
        GATES * nr, GATES * nr, ns * nr, ns * nr,
    ]
    sems = [dma if n is None else dma((n,)) for n in counts]
    whole = pl.BlockSpec(memory_space=pltpu.VMEM)
    out_in, out_w, out_p = pl.pallas_call(
        functools.partial(kernel, ns, nr),
        out_shape=(
            jax.ShapeDtypeStruct((T, DI), BF16),
            jax.ShapeDtypeStruct(weight_t.shape, F32),
            jax.ShapeDtypeStruct((6, H), F32),
        ),
        in_specs=[whole] * 7,
        out_specs=(whole,) * 3,
        scratch_shapes=scratch + sems,
        compiler_params=pltpu.CompilerParams(
            collective_id=0, has_side_effects=True, vmem_limit_bytes=56 * 1024 * 1024
        ),
    )(inputs[0], weight_t, states[0], doc_ids, recur, bias, out_grad[0])
    return out_in[None], out_w, out_p


def fits(ns, nr, inputs, weight_t, states):
    parts, L, DI = inputs.shape
    H = states.shape[2]
    return (
        parts == nr
        and ns % 8 == 0
        and nr % 2 == 0
        and H % (ns * 128) == 0
        and DI % (nr * 128) == 0
        and L % (ns * 128) == 0
        and L * DI <= 1 << 21
    )


def solution(mesh):
    ns, nr = mesh.shape["seq"], mesh.shape["rep"]
    placed = (
        P("rep", "seq", None),
        P("seq", "rep"),
        P("rep", "seq", None),
        P("rep", "seq"),
        P(),
        P(),
        P("rep", "seq", None),
    )

    def run(inputs, weight_t, states, doc_ids, recur, bias, out_grad):
        kernelized = fits(ns, nr, inputs, weight_t, states)
        body = functools.partial(by_hidden, ns, nr) if kernelized else by_tokens
        return jax.shard_map(
            body,
            mesh=mesh,
            in_specs=placed,
            out_specs=(P("rep", "seq", None), P("seq", "rep"), P()),
            check_vma=False,
        )(inputs, weight_t, states, doc_ids, recur, bias, out_grad)

    return run
```

time: 493 us -> 100 us (0.20); the launches traced: 488 us -> 100 us
  waiting for transfers between devices: 306 us -> 0 us
  Pallas kernels: 0 us -> 96.4 us
  blocking collectives: 66.9 us -> 0 us
  local copies, waits for them, and re-layouts: 42.2 us -> 3.1 us
  other arithmetic: 25.3 us -> 0 us
  matrix products: 15.8 us -> 0 us
  starting transfers between devices: 15.6 us -> 0 us
  between operations: 15.7 us -> 0.65 us
    reduce_scatter x2 -> x0, waiting for transfers between devices: 208 us -> none  [the longest x1 208 us: local(): lax.psum_scatter(lax.dot_general(grad_pre, feats, (((0,), (0,)), ((), ())...]
    pallas_call x0 -> x1, Pallas kernels: none -> 96.4 us  [by_hidden(): pl.pallas_call(functools.partial(kernel, ns, nr), out_shape=(jax.ShapeDty...]
    all_gather x1 -> x0, waiting for transfers between devices: 94.6 us -> none  [local(): full_weight = lax.all_gather(columns, 'seq', axis=0, tiled=True)]
    psum x1 -> x0, blocking collectives: 39.2 us -> none  [local(): param_grad = lax.psum(stats, ('seq', 'rep')) * normal_factor]
    slice x72 -> x0, local copies, waits for them, and re-layouts: 34.8 us -> none  [the longest x66 33.1 us: local(): lax.associative_scan(compose, (factor, up_rows), reverse=True, axis=1)]
    all_to_all x1 -> x0, blocking collectives: 17.9 us -> none  [local(): lax.all_to_all(adjoint_rows, 'seq', split_axis=1, concat_axis=0, tiled=True)]
    dot_general x3 -> x0, matrix products: 15.8 us -> none  [the longest x1 6.35 us: local(): lax.dot_general(grad_pre, feats, (((0,), (0,)), ((), ())), preferred_elem...]
    all_to_all x2 -> x0, starting transfers between devices: 10.5 us -> none  [the longest x1 5.71 us: local(): lax.all_to_all(upstream.T, 'seq', split_axis=0, concat_axis=1, tiled=True)]
  transfers between devices with their start and end apart: 7 -> 0, of which waited for: 3 -> 0; matrix products, arithmetic and copies ran while one was open for 4% -> 0% of each run, Pallas kernels for 0% -> 0%
where the time goes in v1:
time: 100 us
  Pallas kernels  96.4 us (96%)
  local copies, waits for them, and re-layouts  3.1 us (3%)
    pallas_call x1, Pallas kernels, by_hidden(): pl.pallas_call(functools.partial(kernel, ns, nr), out_shape=(jax.ShapeDty...  96.4 us
    unnamed x7, local copies, waits for them, and re-layouts  3.1 us

profile of v1, /device:TPU:27, one launch (start us, length us, event | category | flops | bytes accessed | tf_op | source)
XLA Modules:
  0.0 100.1 jit_solution(11568423340805104037)
XLA Ops:
  0.6 96.4 %shard_map.94 = (bf16[128,1024]{1,0:T(8,128)(2,1)}, f32[384,256]{1,0:T(8,128)}, f32[6,1024]{1,0:T(8,128)}) custom-call(bf16[128,1024]{1,0:T(8,128)(2,1)} %bitcast.6, bf16[384,256]{1,0:T(8,128)(2,1)} %weight.1, f32[128,1024]{1,0:T(8,128)} %bitcast.4, s32[1,128]{1,0:T(1,128)} %ids.1, f32[3,1024]{1,0:T(4,128)} %recur.1, f32[3,1024]{1,0:T(4,128)} %bias.1, ...), custom_call_target="tpu_custom_call" | custom-call | tf_op jit(solution)/shard_map/pallas_call | solution.py:453
  97.0 0.0 copy-start
  97.0 1.7 %copy.13 = bf16[1,128,1024]{2,1,0:T(8,128)(2,1)} copy(bf16[1,128,1024]{2,1,0:T(8,128)(2,1)} %bitcast.5) | data formatting | bytes 524288
  98.8 0.0 copy-done
  98.8 0.0 copy-start.1
  98.8 0.7 copy.14
  99.5 0.0 copy-done.1
  99.5 0.6 copy.15
Async XLA Ops:
  97.0 1.7 %copy-start = (f32[384,256]{1,0:T(8,128)S(1)}, f32[384,256]{1,0:T(8,128)}, u32[]{:S(2)}) copy-start(f32[384,256]{1,0:T(8,128)} %get-tuple-element.13) | copy-start | bytes 1179652
  98.8 0.8 copy-start.1

commit v2 on v1

v2 whole, which is shorter than its diff:
```python
import functools
import math

import jax
import jax.numpy as jnp
from jax import lax
from jax.experimental import pallas as pl
from jax.experimental.pallas import tpu as pltpu
from jax.sharding import PartitionSpec as P

F32 = jnp.float32
BF16 = jnp.bfloat16
GATES = 3


def shifted(block, axis, distance):
    devices = range(lax.axis_size(axis))
    route = [(i - distance, i) for i in devices if i - distance in devices]
    return lax.ppermute(block, axis, route)


def compose(earlier, later):
    return (later[0] * earlier[0], later[1] + later[0] * earlier[1])


def by_tokens(inputs, weight_t, states, doc_ids, recur, bias, out_grad):
    feats = inputs[0]
    hidden_now = states[0]
    ids_float = doc_ids[0].astype(F32)
    count = feats.shape[0]
    width = hidden_now.shape[1]
    columns = lax.all_gather(weight_t, "rep", axis=1, tiled=True)
    contract_last = (((1,), (1,)), ((), ()))
    full_weight = lax.all_gather(columns, "seq", axis=0, tiled=True)
    preact = lax.dot_general(feats, full_weight, contract_last, preferred_element_type=F32)
    tail_state, tail_id = shifted((hidden_now[-1:], ids_float[-1:]), "seq", 1)
    first_same = jnp.where(
        (ids_float[0] == tail_id[0]) & (lax.axis_index("seq") > 0), 1.0, 0.0
    ).astype(F32)
    same = jnp.concatenate([first_same[None], (ids_float[1:] == ids_float[:-1]).astype(F32)])
    prior = jnp.concatenate([tail_state, hidden_now[:-1]], 0) * same[:, None]
    gate_z = jax.nn.sigmoid(preact[:, :width] + recur[0] * prior + bias[0])
    gate_r = jax.nn.sigmoid(preact[:, width : 2 * width] + recur[1] * prior + bias[1])
    gate_c = jnp.tanh(preact[:, 2 * width :] + recur[2] * gate_r * prior + bias[2])
    jacobian = same[:, None] * (
        1.0
        - gate_z
        + (gate_c - prior) * gate_z * (1.0 - gate_z) * recur[0]
        + gate_z
        * (1.0 - gate_c * gate_c)
        * recur[2]
        * (gate_r + prior * gate_r * (1.0 - gate_r) * recur[1])
    )
    upstream = out_grad[0].astype(F32)
    jac_rows, up_rows = (
        lax.all_to_all(jacobian.T, "seq", split_axis=0, concat_axis=1, tiled=True),
        lax.all_to_all(upstream.T, "seq", split_axis=0, concat_axis=1, tiled=True),
    )
    factor = jnp.concatenate([jac_rows[:, 1:], jnp.zeros((jac_rows.shape[0], 1), F32)], 1)
    _, adjoint_rows = lax.associative_scan(compose, (factor, up_rows), reverse=True, axis=1)
    adjoint = lax.all_to_all(adjoint_rows, "seq", split_axis=1, concat_axis=0, tiled=True).T
    grad_z = adjoint * (gate_c - prior) * gate_z * (1.0 - gate_z)
    grad_c = adjoint * gate_z * (1.0 - gate_c * gate_c)
    grad_r = grad_c * recur[2] * prior * gate_r * (1.0 - gate_r)
    grad_pre = jnp.concatenate([grad_z, grad_r, grad_c], 1).astype(BF16)
    input_grad = jnp.dot(grad_pre, full_weight, preferred_element_type=F32)
    tokens_all = count * inputs.shape[0] * lax.axis_size("seq") * lax.axis_size("rep")
    normal_factor = 1.0 / math.sqrt(tokens_all)
    row_share = lax.psum_scatter(
        lax.dot_general(grad_pre, feats, (((0,), (0,)), ((), ())), preferred_element_type=F32),
        "seq",
        scatter_dimension=0,
        tiled=True,
    )
    weight_grad = (
        lax.psum_scatter(row_share.astype(BF16), "rep", scatter_dimension=1, tiled=True).astype(F32)
        * normal_factor
    )
    stats = jnp.stack(
        [
            grad_z.sum(0),
            grad_r.sum(0),
            grad_c.sum(0),
            (grad_z * prior).sum(0),
            (grad_r * prior).sum(0),
            (grad_c * gate_r * prior).sum(0),
        ]
    )
    param_grad = lax.psum(stats, ("seq", "rep")) * normal_factor
    return (input_grad.astype(BF16)[None], weight_grad, param_grad)


def kernel(
    ns, nr, feats, weight, states, ids, recur, bias, upstream,
    out_in, out_w, out_p,
    pay_src, pay, ids_src, ids_all, tail_src, tail_in, x_all, w_all, prev, ids_col, up, jac,
    co_z, co_r, co_c, rprior, prior_all,
    scan_a, scan_b, carry, seg_out, seg_in, lam, grads, part_out, part_in, part_keep, fin_out, fin_in,
    wg_out, wg_in, st_out, st_in,
    x_s0, x_sx, x_sy, x_sd, x_r, w_s, w_r, p_s, p_r, i_s, i_r, e_s, e_r, c_s, c_r, d_s, d_r, f_s, f_r,
    g_s, g_r, t_s, t_r,
):
    T, DI = feats.shape
    H = states.shape[1]
    nh, nz, nx = 2 * nr, ns // 2, nr // 2
    hb, cw = H // nh, DI // nr
    s, r = lax.axis_index("seq"), lax.axis_index("rep")
    z, y, x, c = s // 2, s % 2, r // 2, r % 2
    k = 2 * r + y
    me = s * nr + r
    unsent = []

    def place(a, b):
        return {"seq": a, "rep": b}

    def at(plane, j):
        return place(2 * plane + j % 2, j // 2)

    def send(src, dst, ssem, rsem, where):
        pltpu.make_async_remote_copy(
            src_ref=src, dst_ref=dst, send_sem=ssem, recv_sem=rsem,
            device_id=where, device_id_type=pl.DeviceIdType.MESH,
        ).start()

    def local(src, dst, rsem):
        pltpu.make_async_copy(src, dst, rsem).start()

    def landed(dst, sem):
        pltpu.make_async_copy(dst, dst, sem).wait()

    def send_if(allowed, src, dst, ssem, rsem, where):
        @pl.when(allowed)
        def _():
            send(src, dst, ssem, rsem, where)

        unsent.append((allowed, src, ssem))

    def send_or_local(src, dst, ssem, rsem, where, here):
        send_if(jnp.logical_not(here), src, dst, ssem, rsem, where)

        @pl.when(here)
        def _():
            local(src, dst, rsem)

    def rows(ref, block, count):
        return ref.at[pl.ds(pl.multiple_of(block * count, count), count), :]

    for j in range(nh):
        pay_src[j, :, :hb] = states[:, j * hb : (j + 1) * hb].astype(BF16)
        pay_src[j, :, hb:] = upstream[:, j * hb : (j + 1) * hb]
        tail_src[j, 0:8, :] = states[T - 8 : T, j * hb : (j + 1) * hb]
        tail_src[j, 8:16, :] = jnp.broadcast_to(ids[0:1, T - 1 : T].astype(F32), (8, hb))
    ids_src[...] = jnp.broadcast_to(ids[...].astype(F32), ids_src.shape)

    barrier = pltpu.get_barrier_semaphore()

    def greet(d, _):
        @pl.when(d != me)
        def _():
            pl.semaphore_signal(
                barrier, inc=1, device_id=place(d // nr, d % nr), device_id_type=pl.DeviceIdType.MESH
            )

        return 0

    lax.fori_loop(0, ns * nr, greet, 0)
    pl.semaphore_wait(barrier, ns * nr - 1)

    partner = place(s, r + 1 - 2 * c)
    local(feats, rows(x_all, k, T), x_s0)

    def share(step, src, dx, dy):
        x0, y0 = (x + dx) % nx, (y + dy) % 2
        slot = 2 * (2 * x0 + c) + y0
        dst = rows(x_all, slot, T)
        src = dst if src is None else src
        if dy == 0 or dx == 0:
            for other in range(1, nx):
                if dx == 0:
                    allowed = True if dy == 0 else c == 0
                    send_if(
                        allowed, src, dst, x_sx.at[step * nx + other], x_r.at[slot],
                        place(s, 2 * ((x + other) % nx) + c),
                    )
            if dy == 0:
                allowed = True if dx == 0 else c == 1
                send_if(allowed, src, dst, x_sy.at[step], x_r.at[slot], place(2 * z + 1 - y, r))
        send_if(True, src, dst, x_sd.at[step], x_r.at[slot], partner)

    share(0, feats, 0, 0)

    for i in range(GATES):
        b = GATES * s + i
        g, j = b // nh, b % nh
        dst = w_all.at[
            pl.ds(pl.multiple_of(g * hb, hb), hb), pl.ds(pl.multiple_of(r * cw, cw), cw)
        ]
        for step in range(nz):
            plane = (z + step) % nz
            here = jnp.logical_and(step == 0, j == k)
            send_or_local(
                weight.at[i * hb : (i + 1) * hb, :], dst, w_s.at[i * nz + step],
                w_r.at[g * nr + r], at(plane, j), here,
            )
    for j in range(nh):
        send_or_local(ids_src, ids_all.at[k], i_s.at[j], i_r.at[k], at(z, j), k == j)
        send_or_local(pay_src.at[j], pay.at[k], p_s.at[j], p_r.at[k], at(z, j), k == j)
        send_if(
            jnp.logical_and(y == 1, z < nz - 1), tail_src.at[j], tail_in.at[r], e_s.at[j], e_r.at[r],
            at(z + 1, j),
        )

    hops = [(dx, dy) for dx in range(nx) for dy in range(2)]
    hops.sort(key=lambda hop: (hop[0] > 0) + hop[1])
    for step, (dx, dy) in enumerate(hops):
        if step > 0:
            slot = 2 * (2 * ((x + dx) % nx) + c) + (y + dy) % 2
            landed(rows(x_all, slot, T), x_r.at[slot])
            share(step, None, dx, dy)

    stride = T + 8
    for m in range(nh):
        base = m * stride + 8
        landed(ids_all.at[m], i_r.at[m])
        landed(pay.at[m], p_r.at[m])
        prev[base : base + T, :] = pay[m, :, :hb].astype(F32)
        up[m * T : (m + 1) * T, :] = pay[m, :, hb:].astype(F32)
        ids_col[base : base + T, :] = jnp.broadcast_to(ids_all[m, 0:1, :], (hb, T)).T
        if m % 2:
            before = base - stride + T
            prev[base - 8 : base, :] = prev[before - 8 : before, :]
            ids_col[base - 8 : base, :] = ids_col[before - 8 : before, :]
        else:

            @pl.when(z > 0)
            def _():
                landed(tail_in.at[m // 2], e_r.at[m // 2])
                prev[base - 8 : base, :] = tail_in[m // 2, 0:8, :]
                ids_col[base - 8 : base, :] = tail_in[m // 2, 8:16, :]

            @pl.when(z == 0)
            def _():
                prev[base - 8 : base, :] = jnp.zeros((8, hb), F32)
                ids_col[base - 8 : base, :] = jnp.full((8, hb), -1.0, F32)

    for g in range(GATES):
        for col in range(nr):
            landed(
                w_all.at[g * hb : (g + 1) * hb, col * cw : (col + 1) * cw], w_r.at[g * nr + col]
            )
    landed(rows(x_all, k, T), x_s0)
    for x0 in range(nx):
        for y0 in range(2):
            slot = 2 * (2 * x0 + 1 - c) + y0
            landed(rows(x_all, slot, T), x_r.at[slot])

    group = pl.ds(pl.multiple_of(k * hb, hb), hb)
    rz, rr, rc = (recur[i : i + 1, group] for i in range(GATES))
    bz, br, bc = (bias[i : i + 1, group] for i in range(GATES))
    for m in range(nh):
        span = slice(m * T, (m + 1) * T)
        base = m * stride + 8
        pre = lax.dot_general(
            x_all[span, :], w_all[...], (((1,), (1,)), ((), ())), preferred_element_type=F32
        )
        same = jnp.where(
            ids_col[base : base + T, :] == ids_col[base - 1 : base - 1 + T, :], 1.0, 0.0
        )
        prior = prev[base - 1 : base - 1 + T, :] * same
        gz = jax.nn.sigmoid(pre[:, :hb] + rz * prior + bz)
        gr = jax.nn.sigmoid(pre[:, hb : 2 * hb] + rr * prior + br)
        rp = gr * prior
        gc = jnp.tanh(pre[:, 2 * hb :] + rc * rp + bc)
        az = (gc - prior) * gz * (1.0 - gz)
        ac = gz * (1.0 - gc * gc)
        slope = rp * (1.0 - gr)
        acr = ac * rc
        co_z[span, :] = az
        co_c[span, :] = ac
        co_r[span, :] = acr * slope
        rprior[span, :] = rp
        prior_all[span, :] = prior
        jac[span, :] = same * (1.0 - gz + az * rz + acr * (gr + slope * rr))

    def back(i, state):
        a, b = state
        t = T - 1 - i
        f = jac[pl.ds(t, nh, stride=T), :]
        b = b + up[pl.ds(t, nh, stride=T), :]
        scan_a[t] = a
        scan_b[t] = b
        return f * a, f * b

    a, b = lax.fori_loop(0, T, back, (jnp.ones((nh, hb), F32), jnp.zeros((nh, hb), F32)), unroll=8)
    seg_out[...] = jnp.zeros(seg_out.shape, F32)
    for o in range(nr):
        first, second = slice(2 * o, 2 * o + 1), slice(2 * o + 1, 2 * o + 2)
        seg_out[0, o : o + 1, :] = a[first, :] * a[second, :]
        seg_out[1, o : o + 1, :] = b[first, :] + a[first, :] * b[second, :]
    for plane in range(nz - 1):
        send_if(plane < z, seg_out, seg_in.at[z], c_s.at[plane], c_r.at[z], at(plane, k))
    carry[...] = jnp.zeros(carry.shape, F32)
    for plane in reversed(range(1, nz)):

        @pl.when(plane > z)
        def _():
            landed(seg_in.at[plane], c_r.at[plane])
            carry[0:nr, :] = seg_in[plane, 1, 0:nr, :] + seg_in[plane, 0, 0:nr, :] * carry[0:nr, :]

    into = carry[0:nr, :]
    carry_rows = []
    for o in range(nr):
        later = into[o : o + 1, :]
        second = slice(2 * o + 1, 2 * o + 2)
        carry_rows += [b[second, :] + a[second, :] * later, later]
    carried = jnp.concatenate(carry_rows, 0)

    def finish(t, _):
        lam[pl.ds(t, nh, stride=T), :] = scan_b[t] + scan_a[t] * carried
        return 0

    lax.fori_loop(0, T, finish, 0, unroll=8)

    sums = [jnp.zeros((1, hb), F32) for _ in range(6)]
    for m in range(nh):
        span = slice(m * T, (m + 1) * T)
        prior = prior_all[span, :]
        adj = lam[span, :]
        grad_z = adj * co_z[span, :]
        grad_r = adj * co_r[span, :]
        grad_c = adj * co_c[span, :]
        grads[span, :hb] = grad_z.astype(BF16)
        grads[span, hb : 2 * hb] = grad_r.astype(BF16)
        grads[span, 2 * hb :] = grad_c.astype(BF16)
        terms = (grad_z, grad_r, grad_c, grad_z * prior, grad_r * prior, grad_c * rprior[span, :])
        sums = [total + jnp.sum(term, 0, keepdims=True) for total, term in zip(sums, terms)]
    for i in range(6):
        st_out[i : i + 1, :] = sums[i]
    st_out[6:8, :] = jnp.zeros((2, hb), F32)

    for g in range(GATES):
        wg_out[g] = lax.dot_general(
            grads[:, g * hb : (g + 1) * hb], x_all[...], (((0,), (0,)), ((), ())),
            preferred_element_type=F32,
        ).astype(BF16)
        b = g * nh + k
        owner, i = b // GATES, b % GATES
        for col in range(nr):
            here = jnp.logical_and(owner == s, r == col)
            send_or_local(
                wg_out.at[g, :, col * cw : (col + 1) * cw], wg_in.at[z * GATES + i],
                g_s.at[g * nr + col], g_r.at[z * GATES + i], place(owner, col), here,
            )

    chips = [(x0, y0) for x0 in range(nx) for y0 in range(2)]
    for n, (x0, y0) in enumerate(chips):
        part_out[n] = jnp.dot(
            rows(grads, 2 * (2 * x0 + 1 - c) + y0, T)[...], w_all[...], preferred_element_type=F32
        ).astype(BF16)
        send_if(True, part_out.at[n], part_in.at[n], d_s.at[n], d_r.at[n], partner)
    for n, (x0, y0) in enumerate(chips):
        part_keep[n] = jnp.dot(
            rows(grads, 2 * (2 * x0 + c) + y0, T)[...], w_all[...], preferred_element_type=F32
        )
    chip = 2 * x + y
    for n, (x0, y0) in enumerate(chips):
        landed(part_in.at[n], d_r.at[n])
        fin_out[n] = (part_keep[n] + part_in[n].astype(F32)).astype(BF16)
        send_or_local(
            fin_out.at[n], fin_in.at[chip], f_s.at[n], f_r.at[chip],
            place(2 * z + y0, 2 * x0 + c), chip == n,
        )

    slot = k * nz + z
    st_in[slot] = st_out[...]

    def tell(d, _):
        @pl.when(d != me)
        def _():
            send(st_out, st_in.at[slot], t_s.at[d], t_r.at[slot], place(d // nr, d % nr))

        return 0

    lax.fori_loop(0, ns * nr, tell, 0)

    scale = 1.0 / math.sqrt(ns * nr * T)

    def heard(d, _):
        @pl.when(d != slot)
        def _():
            landed(st_in.at[d], t_r.at[d])

        return 0

    lax.fori_loop(0, ns * nr, heard, 0)
    for j in range(nh):
        total = st_in[j * nz]
        for other in range(1, nz):
            total = total + st_in[j * nz + other]
        out_p[:, j * hb : (j + 1) * hb] = total[:6] * scale

    total = None
    for n in range(len(chips)):
        landed(fin_in.at[n], f_r.at[n])
        term = fin_in[n].astype(F32)
        total = term if total is None else total + term
    out_in[...] = total.astype(BF16)

    for i in range(GATES):
        total = None
        for other in range(nz):
            landed(wg_in.at[other * GATES + i], g_r.at[other * GATES + i])
            term = wg_in[other * GATES + i].astype(F32)
            total = term if total is None else total + term
        out_w[i * hb : (i + 1) * hb, :] = total * scale

    def told(d, _):
        @pl.when(d != me)
        def _():
            landed(st_out, t_s.at[d])

        return 0

    lax.fori_loop(0, ns * nr, told, 0)
    for sent, src, sem in unsent:
        if sent is True:
            landed(src, sem)
        else:

            @pl.when(sent)
            def _():
                landed(src, sem)


def by_hidden(ns, nr, inputs, weight_t, states, doc_ids, recur, bias, out_grad):
    T, DI = inputs.shape[1:]
    H = states.shape[2]
    nh, nz, nx = 2 * nr, ns // 2, nr // 2
    hb, cw = H // nh, DI // nr
    L = nh * T
    vm = pltpu.VMEM
    scratch = [
        vm((nh, T, 2 * hb), BF16),
        vm((nh, T, 2 * hb), BF16),
        vm((8, T), F32),
        vm((nh, 8, T), F32),
        vm((nh, 16, hb), F32),
        vm((nr, 16, hb), F32),
        vm((L, DI), BF16),
        vm((GATES * hb, DI), BF16),
        vm((L + 8 * nh, hb), F32),
        vm((L + 8 * nh, hb), F32),
        vm((L, hb), F32),
        vm((L, hb), F32),
        vm((L, hb), F32),
        vm((L, hb), F32),
        vm((L, hb), F32),
        vm((L, hb), F32),
        vm((L, hb), F32),
        vm((T, nh, hb), F32),
        vm((T, nh, hb), F32),
        vm((nh, hb), F32),
        vm((2, 8, hb), F32),
        vm((nz, 2, 8, hb), F32),
        vm((L, hb), F32),
        vm((L, GATES * hb), BF16),
        vm((nr, T, DI), BF16),
        vm((nr, T, DI), BF16),
        vm((nr, T, DI), F32),
        vm((nr, T, DI), BF16),
        vm((nr, T, DI), BF16),
        vm((GATES, hb, DI), BF16),
        vm((nz * GATES, hb, cw), BF16),
        vm((8, hb), F32),
        vm((ns * nr, 8, hb), F32),
    ]
    dma = pltpu.SemaphoreType.DMA
    counts = [
        None, nr * nx, nr, nr, nh, GATES * nz, GATES * nr, nh, nh, nh, nh, nh, nr, nz, nz, nr, nr, nr, nr,
        GATES * nr, GATES * nz, ns * nr, ns * nr,
    ]
    sems = [dma if n is None else dma((n,)) for n in counts]
    whole = pl.BlockSpec(memory_space=pltpu.VMEM)
    out_in, out_w, out_p = pl.pallas_call(
        functools.partial(kernel, ns, nr),
        out_shape=(
            jax.ShapeDtypeStruct((T, DI), BF16),
            jax.ShapeDtypeStruct(weight_t.shape, F32),
            jax.ShapeDtypeStruct((6, H), F32),
        ),
        in_specs=[whole] * 7,
        out_specs=(whole,) * 3,
        scratch_shapes=scratch + sems,
        compiler_params=pltpu.CompilerParams(
            collective_id=0, has_side_effects=True, vmem_limit_bytes=56 * 1024 * 1024
        ),
    )(inputs[0], weight_t, states[0], doc_ids, recur, bias, out_grad[0])
    return out_in[None], out_w, out_p


def fits(ns, nr, inputs, weight_t, states):
    parts, L, DI = inputs.shape
    H = states.shape[2]
    return (
        parts == nr
        and ns == 2 * nr
        and ns % 8 == 0
        and ns == 8
        and H % (ns * 128) == 0
        and DI % (nr * 128) == 0
        and L % (ns * 128) == 0
        and L * DI <= 1 << 21
    )


def solution(mesh):
    ns, nr = mesh.shape["seq"], mesh.shape["rep"]
    placed = (
        P("rep", "seq", None),
        P("seq", "rep"),
        P("rep", "seq", None),
        P("rep", "seq"),
        P(),
        P(),
        P("rep", "seq", None),
    )

    def run(inputs, weight_t, states, doc_ids, recur, bias, out_grad):
        kernelized = fits(ns, nr, inputs, weight_t, states)
        body = functools.partial(by_hidden, ns, nr) if kernelized else by_tokens
        return jax.shard_map(
            body,
            mesh=mesh,
            in_specs=placed,
            out_specs=(P("rep", "seq", None), P("seq", "rep"), P()),
            check_vma=False,
        )(inputs, weight_t, states, doc_ids, recur, bias, out_grad)

    return run
```

time: 100 us -> 76.5 us (0.77); the launches traced: 100 us -> 75.4 us
  Pallas kernels: 96.4 us -> 71.7 us
    pallas_call x1, Pallas kernels: 96.4 us -> 71.7 us  [by_hidden(): pl.pallas_call(functools.partial(kernel, ns, nr), out_shape=(jax.ShapeDty...]
where the time goes in v2:
time: 76.5 us; the launch traced here: 75.4 us
  Pallas kernels  71.7 us (94%)
  local copies, waits for them, and re-layouts  3.1 us (4%)
    pallas_call x1, Pallas kernels, by_hidden(): pl.pallas_call(functools.partial(kernel, ns, nr), out_shape=(jax.ShapeDty...  71.7 us
    unnamed x7, local copies, waits for them, and re-layouts  3.1 us

profile of v2, /device:TPU:27, one launch (start us, length us, event | category | flops | bytes accessed | tf_op | source)
XLA Modules:
  0.0 75.4 jit_solution(17698740123519689427)
XLA Ops:
  0.6 71.7 %shard_map.94 = (bf16[128,1024]{1,0:T(8,128)(2,1)}, f32[384,256]{1,0:T(8,128)}, f32[6,1024]{1,0:T(8,128)}) custom-call(bf16[128,1024]{1,0:T(8,128)(2,1)} %bitcast.6, bf16[384,256]{1,0:T(8,128)(2,1)} %weight.1, f32[128,1024]{1,0:T(8,128)} %bitcast.4, s32[1,128]{1,0:T(1,128)} %ids.1, f32[3,1024]{1,0:T(4,128)} %recur.1, f32[3,1024]{1,0:T(4,128)} %bias.1, ...), custom_call_target="tpu_custom_call" | custom-call | tf_op jit(solution)/shard_map/pallas_call | solution.py:484
  72.3 0.0 copy-start
  72.3 1.7 %copy.13 = bf16[1,128,1024]{2,1,0:T(8,128)(2,1)} copy(bf16[1,128,1024]{2,1,0:T(8,128)(2,1)} %bitcast.5) | data formatting | bytes 524288
  74.0 0.0 copy-done
  74.0 0.0 copy-start.1
  74.0 0.7 copy.14
  74.8 0.0 copy-done.1
  74.8 0.6 copy.15
Async XLA Ops:
  72.3 1.7 %copy-start = (f32[384,256]{1,0:T(8,128)S(1)}, f32[384,256]{1,0:T(8,128)}, u32[]{:S(2)}) copy-start(f32[384,256]{1,0:T(8,128)} %get-tuple-element.13) | copy-start | bytes 1179652
  74.0 0.8 %copy-start.1 = (f32[6,1024]{1,0:T(8,128)S(1)}, f32[6,1024]{1,0:T(8,128)}, u32[]{:S(2)}) copy-start(f32[6,1024]{1,0:T(8,128)} %get-tuple-element.14) | copy-start | bytes 73732

commit v3 on v2

--- a/solution.py
+++ b/solution.py
@@ -145,6 +145,18 @@
     def rows(ref, block, count):
         return ref.at[pl.ds(pl.multiple_of(block * count, count), count), :]
 
+    barrier = pltpu.get_barrier_semaphore()
+
+    def greet(d, _):
+        @pl.when(d != me)
+        def _():
+            pl.semaphore_signal(
+                barrier, inc=1, device_id=place(d // nr, d % nr), device_id_type=pl.DeviceIdType.MESH
+            )
+
+        return 0
+
+    lax.fori_loop(0, ns * nr, greet, 0)
     for j in range(nh):
         pay_src[j, :, :hb] = states[:, j * hb : (j + 1) * hb].astype(BF16)
         pay_src[j, :, hb:] = upstream[:, j * hb : (j + 1) * hb]
@@ -152,20 +164,22 @@
         tail_src[j, 8:16, :] = jnp.broadcast_to(ids[0:1, T - 1 : T].astype(F32), (8, hb))
     ids_src[...] = jnp.broadcast_to(ids[...].astype(F32), ids_src.shape)
 
-    barrier = pltpu.get_barrier_semaphore()
-
-    def greet(d, _):
-        @pl.when(d != me)
-        def _():
-            pl.semaphore_signal(
-                barrier, inc=1, device_id=place(d // nr, d % nr), device_id_type=pl.DeviceIdType.MESH
+    pl.semaphore_wait(barrier, ns * nr - 1)
+
+    steps = sorted(range(nz), key=lambda step: -min(step, nz - step))
+    for step in steps:
+        plane = (z + step) % nz
+        for i in range(GATES):
+            b = GATES * s + i
+            g, j = b // nh, b % nh
+            dst = w_all.at[
+                pl.ds(pl.multiple_of(g * hb, hb), hb), pl.ds(pl.multiple_of(r * cw, cw), cw)
+            ]
+            here = jnp.logical_and(step == 0, j == k)
+            send_or_local(
+                weight.at[i * hb : (i + 1) * hb, :], dst, w_s.at[i * nz + step],
+                w_r.at[g * nr + r], at(plane, j), here,
             )
-
-        return 0
-
-    lax.fori_loop(0, ns * nr, greet, 0)
-    pl.semaphore_wait(barrier, ns * nr - 1)
-
     partner = place(s, r + 1 - 2 * c)
     local(feats, rows(x_all, k, T), x_s0)
 
@@ -189,19 +203,6 @@
 
     share(0, feats, 0, 0)
 
-    for i in range(GATES):
-        b = GATES * s + i
-        g, j = b // nh, b % nh
-        dst = w_all.at[
-            pl.ds(pl.multiple_of(g * hb, hb), hb), pl.ds(pl.multiple_of(r * cw, cw), cw)
-        ]
-        for step in range(nz):
-            plane = (z + step) % nz
-            here = jnp.logical_and(step == 0, j == k)
-            send_or_local(
-                weight.at[i * hb : (i + 1) * hb, :], dst, w_s.at[i * nz + step],
-                w_r.at[g * nr + r], at(plane, j), here,
-            )
     for j in range(nh):
         send_or_local(ids_src, ids_all.at[k], i_s.at[j], i_r.at[k], at(z, j), k == j)
         send_or_local(pay_src.at[j], pay.at[k], p_s.at[j], p_r.at[k], at(z, j), k == j)
@@ -338,6 +339,18 @@
         st_out[i : i + 1, :] = sums[i]
     st_out[6:8, :] = jnp.zeros((2, hb), F32)
 
+    slot = k * nz + z
+    st_in[slot] = st_out[...]
+
+    def tell(d, _):
+        @pl.when(d != me)
+        def _():
+            send(st_out, st_in.at[slot], t_s.at[d], t_r.at[slot], place(d // nr, d % nr))
+
+        return 0
+
+    lax.fori_loop(0, ns * nr, tell, 0)
+
     for g in range(GATES):
         wg_out[g] = lax.dot_general(
             grads[:, g * hb : (g + 1) * hb], x_all[...], (((0,), (0,)), ((), ())),
@@ -370,18 +383,6 @@
             fin_out.at[n], fin_in.at[chip], f_s.at[n], f_r.at[chip],
             place(2 * z + y0, 2 * x0 + c), chip == n,
         )
-
-    slot = k * nz + z
-    st_in[slot] = st_out[...]
-
-    def tell(d, _):
-        @pl.when(d != me)
-        def _():
-            send(st_out, st_in.at[slot], t_s.at[d], t_r.at[slot], place(d // nr, d % nr))
-
-        return 0
-
-    lax.fori_loop(0, ns * nr, tell, 0)
 
     scale = 1.0 / math.sqrt(ns * nr * T)
 

time: 76.5 us -> 72.4 us (0.946); the launches traced: 75.4 us -> 72.2 us
  Pallas kernels: 71.7 us -> 68.4 us
    pallas_call x1, Pallas kernels: 71.7 us -> 68.4 us  [by_hidden(): pl.pallas_call(functools.partial(kernel, ns, nr), out_shape=(jax.ShapeDty...]
where the time goes in v3:
time: 72.4 us; the launch traced here: 72.2 us
  Pallas kernels  68.4 us (94%)
  local copies, waits for them, and re-layouts  3.1 us (4%)
    pallas_call x1, Pallas kernels, by_hidden(): pl.pallas_call(functools.partial(kernel, ns, nr), out_shape=(jax.ShapeDty...  68.4 us
    unnamed x7, local copies, waits for them, and re-layouts  3.1 us

profile of v3, /device:TPU:27, one launch (start us, length us, event | category | flops | bytes accessed | tf_op | source)
XLA Modules:
  0.0 72.2 jit_solution(2365252933304439288)
XLA Ops:
  0.6 68.4 %shard_map.94 = (bf16[128,1024]{1,0:T(8,128)(2,1)}, f32[384,256]{1,0:T(8,128)}, f32[6,1024]{1,0:T(8,128)}) custom-call(bf16[128,1024]{1,0:T(8,128)(2,1)} %bitcast.6, bf16[384,256]{1,0:T(8,128)(2,1)} %weight.1, f32[128,1024]{1,0:T(8,128)} %bitcast.4, s32[1,128]{1,0:T(1,128)} %ids.1, f32[3,1024]{1,0:T(4,128)} %recur.1, f32[3,1024]{1,0:T(4,128)} %bias.1, ...), custom_call_target="tpu_custom_call" | custom-call | tf_op jit(solution)/shard_map/pallas_call | solution.py:485
  69.1 0.0 copy-start
  69.1 1.7 %copy.13 = bf16[1,128,1024]{2,1,0:T(8,128)(2,1)} copy(bf16[1,128,1024]{2,1,0:T(8,128)(2,1)} %bitcast.5) | data formatting | bytes 524288
  70.8 0.0 copy-done
  70.8 0.0 copy-start.1
  70.8 0.7 %copy.14 = f32[384,256]{1,0:T(8,128)} copy(f32[384,256]{1,0:T(8,128)S(1)} %copy-done) | data formatting | bytes 786432
  71.5 0.0 copy-done.1
  71.5 0.6 copy.15
Async XLA Ops:
  69.1 1.7 %copy-start = (f32[384,256]{1,0:T(8,128)S(1)}, f32[384,256]{1,0:T(8,128)}, u32[]{:S(2)}) copy-start(f32[384,256]{1,0:T(8,128)} %get-tuple-element.13) | copy-start | bytes 1179652
  70.8 0.8 %copy-start.1 = (f32[6,1024]{1,0:T(8,128)S(1)}, f32[6,1024]{1,0:T(8,128)}, u32[]{:S(2)}) copy-start(f32[6,1024]{1,0:T(8,128)} %get-tuple-element.14) | copy-start | bytes 73732

commit v4 on v3

--- a/solution.py
+++ b/solution.py
@@ -96,7 +96,7 @@
     pay_src, pay, ids_src, ids_all, tail_src, tail_in, x_all, w_all, prev, ids_col, up, jac,
     co_z, co_r, co_c, rprior, prior_all,
     scan_a, scan_b, carry, seg_out, seg_in, lam, grads, part_out, part_in, part_keep, fin_out, fin_in,
-    wg_out, wg_in, st_out, st_in,
+    wg_out, wg_in, st_out, st_in, pre_all,
     x_s0, x_sx, x_sy, x_sd, x_r, w_s, w_r, p_s, p_r, i_s, i_r, e_s, e_r, c_s, c_r, d_s, d_r, f_s, f_r,
     g_s, g_r, t_s, t_r,
 ):
@@ -258,12 +258,13 @@
     group = pl.ds(pl.multiple_of(k * hb, hb), hb)
     rz, rr, rc = (recur[i : i + 1, group] for i in range(GATES))
     bz, br, bc = (bias[i : i + 1, group] for i in range(GATES))
+    pre_all[...] = lax.dot_general(
+        x_all[...], w_all[...], (((1,), (1,)), ((), ())), preferred_element_type=F32
+    )
     for m in range(nh):
         span = slice(m * T, (m + 1) * T)
         base = m * stride + 8
-        pre = lax.dot_general(
-            x_all[span, :], w_all[...], (((1,), (1,)), ((), ())), preferred_element_type=F32
-        )
+        pre = pre_all[span, :]
         same = jnp.where(
             ids_col[base : base + T, :] == ids_col[base - 1 : base - 1 + T, :], 1.0, 0.0
         )
@@ -351,30 +352,36 @@
 
     lax.fori_loop(0, ns * nr, tell, 0)
 
+    wide = lax.dot_general(
+        grads[...], x_all[...], (((0,), (0,)), ((), ())), preferred_element_type=F32
+    )
     for g in range(GATES):
-        wg_out[g] = lax.dot_general(
-            grads[:, g * hb : (g + 1) * hb], x_all[...], (((0,), (0,)), ((), ())),
-            preferred_element_type=F32,
-        ).astype(BF16)
+        wg_out[g] = wide[g * hb : (g + 1) * hb, :].astype(BF16)
+    for n in range(GATES):
+        g = jnp.where(z < nz // 2, GATES - 1 - n, n)
         b = g * nh + k
         owner, i = b // GATES, b % GATES
         for col in range(nr):
             here = jnp.logical_and(owner == s, r == col)
             send_or_local(
                 wg_out.at[g, :, col * cw : (col + 1) * cw], wg_in.at[z * GATES + i],
-                g_s.at[g * nr + col], g_r.at[z * GATES + i], place(owner, col), here,
+                g_s.at[n * nr + col], g_r.at[z * GATES + i], place(owner, col), here,
             )
 
     chips = [(x0, y0) for x0 in range(nx) for y0 in range(2)]
-    for n, (x0, y0) in enumerate(chips):
-        part_out[n] = jnp.dot(
-            rows(grads, 2 * (2 * x0 + 1 - c) + y0, T)[...], w_all[...], preferred_element_type=F32
-        ).astype(BF16)
-        send_if(True, part_out.at[n], part_in.at[n], d_s.at[n], d_r.at[n], partner)
-    for n, (x0, y0) in enumerate(chips):
-        part_keep[n] = jnp.dot(
-            rows(grads, 2 * (2 * x0 + c) + y0, T)[...], w_all[...], preferred_element_type=F32
+    for x0 in range(nx):
+        wide = jnp.dot(
+            rows(grads, 2 * x0 + 1 - c, 2 * T)[...], w_all[...], preferred_element_type=F32
         )
+        for n in (2 * x0, 2 * x0 + 1):
+            part_out[n] = wide[(n % 2) * T : (n % 2 + 1) * T, :].astype(BF16)
+            send_if(True, part_out.at[n], part_in.at[n], d_s.at[n], d_r.at[n], partner)
+    for x0 in range(nx):
+        wide = jnp.dot(
+            rows(grads, 2 * x0 + c, 2 * T)[...], w_all[...], preferred_element_type=F32
+        )
+        for n in (2 * x0, 2 * x0 + 1):
+            part_keep[n] = wide[(n % 2) * T : (n % 2 + 1) * T, :]
     chip = 2 * x + y
     for n, (x0, y0) in enumerate(chips):
         landed(part_in.at[n], d_r.at[n])
@@ -474,6 +481,7 @@
         vm((nz * GATES, hb, cw), BF16),
         vm((8, hb), F32),
         vm((ns * nr, 8, hb), F32),
+        vm((L, GATES * hb), F32),
     ]
     dma = pltpu.SemaphoreType.DMA
     counts = [

time: 72.4 us -> 72.4 us (level)
  the two profiles are of different devices: /device:TPU:27 before, /device:TPU:19 now
where the time goes in v4:
time: 72.4 us; the launch traced here: 72.2 us
  Pallas kernels  68.4 us (94%)
  local copies, waits for them, and re-layouts  3.1 us (4%)
    pallas_call x1, Pallas kernels, by_hidden(): pl.pallas_call(functools.partial(kernel, ns, nr), out_shape=(jax.ShapeDty...  68.4 us
    unnamed x7, local copies, waits for them, and re-layouts  3.1 us

profile of v4, /device:TPU:19, one launch (start us, length us, event | category | flops | bytes accessed | tf_op | source)
XLA Modules:
  0.0 72.2 jit_solution(5071272059274157123)
XLA Ops:
  0.6 68.4 %shard_map.94 = (bf16[128,1024]{1,0:T(8,128)(2,1)}, f32[384,256]{1,0:T(8,128)}, f32[6,1024]{1,0:T(8,128)}) custom-call(bf16[128,1024]{1,0:T(8,128)(2,1)} %bitcast.6, bf16[384,256]{1,0:T(8,128)(2,1)} %weight.1, f32[128,1024]{1,0:T(8,128)} %bitcast.4, s32[1,128]{1,0:T(1,128)} %ids.1, f32[3,1024]{1,0:T(4,128)} %recur.1, f32[3,1024]{1,0:T(4,128)} %bias.1, ...), custom_call_target="tpu_custom_call" | custom-call | tf_op jit(solution)/shard_map/pallas_call | solution.py:493
  69.1 0.0 copy-start
  69.1 1.7 %copy.13 = bf16[1,128,1024]{2,1,0:T(8,128)(2,1)} copy(bf16[1,128,1024]{2,1,0:T(8,128)(2,1)} %bitcast.5) | data formatting | bytes 524288
  70.8 0.0 copy-done
  70.8 0.0 copy-start.1
  70.8 0.7 %copy.14 = f32[384,256]{1,0:T(8,128)} copy(f32[384,256]{1,0:T(8,128)S(1)} %copy-done) | data formatting | bytes 786432
  71.5 0.0 copy-done.1
  71.6 0.6 copy.15
Async XLA Ops:
  69.1 1.7 %copy-start = (f32[384,256]{1,0:T(8,128)S(1)}, f32[384,256]{1,0:T(8,128)}, u32[]{:S(2)}) copy-start(f32[384,256]{1,0:T(8,128)} %get-tuple-element.13) | copy-start | bytes 1179652
  70.8 0.8 %copy-start.1 = (f32[6,1024]{1,0:T(8,128)S(1)}, f32[6,1024]{1,0:T(8,128)}, u32[]{:S(2)}) copy-start(f32[6,1024]{1,0:T(8,128)} %get-tuple-element.14) | copy-start | bytes 73732
